TPU v7x, 32 devices: a whole 2x2x4 slice. The times are simulated.
32 devices in a mesh: groups: 2 (over y), ep: 16 (over z, x, core).
Axes of the slice: x: 2, y: 2, z: 4, core: 2. Of those that a mesh axis runs over, the one named last changes fastest.
Arguments:
- tokens: bfloat16 [128, 7168], P(('groups', 'ep')), parts along dimension 0, may hold values from -6 to 6
- routes: int32 [128, 8], P(('groups', 'ep')), parts along dimension 0, may hold values from 0 to 15, as said below
- gates: float32 [128, 8], P(('groups', 'ep')), parts along dimension 0, may hold values from 0.05 to 0.6
- gate_weight: bfloat16 [7168, 32768], P(None, 'ep'), may hold values from -0.0625 to 0.0625
- up_weight: bfloat16 [7168, 32768], P(None, 'ep'), may hold values from -0.0625 to 0.0625
- down_weight: bfloat16 [32768, 7168], P('ep'), may hold values from -0.125 to 0.125
Outputs:
- mixed: bfloat16 [128, 7168], P(('groups', 'ep')), parts along dimension 0
There are 2 independent parts, one for each index of `groups`. A program takes and returns all parts, laid end to end along the dimension named above; an argument that names none is the same for every part. Nothing has to cross between parts.
Inputs may be any that keep to these rules, and one draw needn't show every extreme that they name: `routes`: each token names 8 different experts. Among the 4 tokens of one device no expert is named by more than 3 of them, and in every draw one expert is named by exactly 3 tokens of every device.
All inputs are finite; a program needn't handle non-finite values.
Results may differ from a plain program's by a relative error of at most 0.0085.
Values may be sent and summed in bfloat16 or wider, within the bound.
No kernel may reach another device: no remote copies, remote signals or barrier semaphores. Data moves between devices by JAX's collectives and lax.ppermute only.
A program may use at most 128 MiB of HBM per device.

v0:
```python
import jax
import jax.numpy as jnp
from jax import lax
from jax.sharding import PartitionSpec as P

EXPERTS = 16
CAP = 3


def expert_forward(block_in, gate_weight, up_weight, down_weight):
    senders, slot_count, model_width = block_in.shape
    flat_rows = block_in.reshape(senders * slot_count, model_width)
    gate_act = jnp.dot(flat_rows, gate_weight, preferred_element_type=jnp.float32)
    up_act = jnp.dot(flat_rows, up_weight, preferred_element_type=jnp.float32)
    hidden = (jax.nn.silu(gate_act) * up_act).astype(jnp.bfloat16)
    result = jnp.dot(hidden, down_weight, preferred_element_type=jnp.float32)
    return result.reshape(senders, slot_count, model_width)


def shards(tokens, routes, gates, gate_weight, up_weight, down_weight):
    tok_rows, model_width = tokens.shape
    devices_ep = lax.axis_size("ep")
    split_count = devices_ep // EXPERTS
    expert_ids = jnp.arange(EXPERTS, dtype=jnp.int32)
    member = routes[:, :, None] == expert_ids[None, None, :]
    chosen = jnp.any(member, axis=1).astype(jnp.int32)
    gate_share = jnp.sum(jnp.where(member, gates[:, :, None], 0.0), axis=1)
    slot_place = jnp.cumsum(chosen, axis=0) - chosen
    slot_ids = jnp.arange(CAP, dtype=jnp.int32)
    slot_pick = (chosen[:, :, None] == 1) & (slot_place[:, :, None] == slot_ids[None, None, :])
    selector = jnp.transpose(slot_pick, (1, 2, 0)).astype(jnp.bfloat16)
    mix_weight = jnp.where(slot_pick, gate_share[:, :, None], 0.0)
    packed = jnp.einsum("ect,td->ecd", selector, tokens, preferred_element_type=jnp.float32).astype(
        jnp.bfloat16
    )
    outgoing = jnp.broadcast_to(packed[:, None], (EXPERTS, split_count, CAP, model_width)).reshape(
        devices_ep, CAP, model_width
    )
    partial_value = expert_forward(
        lax.all_to_all(outgoing, "ep", split_axis=0, concat_axis=0, tiled=True),
        gate_weight,
        up_weight,
        down_weight,
    )
    returned = lax.all_to_all(partial_value, "ep", split_axis=0, concat_axis=0, tiled=True)
    summed = returned.reshape(EXPERTS, split_count, CAP, model_width).sum(axis=1)
    mixed = jnp.einsum("tec,ecd->td", mix_weight, summed, precision=lax.Precision.HIGHEST)
    return mixed.astype(jnp.bfloat16)


def solution(mesh):
    placed = (
        P(("groups", "ep"), None),
        P(("groups", "ep"), None),
        P(("groups", "ep"), None),
        P(None, "ep"),
        P(None, "ep"),
        P("ep", None),
    )
    return jax.shard_map(
        shards, mesh=mesh, in_specs=placed, out_specs=P(("groups", "ep"), None), check_vma=False
    )
```

profile of v0, /device:TPU:15, one launch (start us, length us, event | category | flops | bytes accessed | tf_op | source)
XLA Modules:
  0.0 114.1 jit_solution(17393039308408811121)
XLA Ops:
  0.0 0.0 copy-start
  0.0 0.8 fusion.11
  0.8 0.0 copy-done
  0.8 0.4 convolution_convert_fusion
  1.3 0.6 copy.12
  1.9 28.3 %all_to_all.10 = bf16[16,3,7168]{2,1,0:T(4,128)(2,1)S(1)} all-to-all(bf16[16,3,7168]{2,1,0:T(4,128)(2,1)S(1)} %copy.12), channel_id=1, replica_groups=mesh['groups'=2,'ep'=16] {'ep'}, dimensions={0} | all-to-all | bytes 1376256 | tf_op jit(solution)/shard_map/all_to_all | solution.py:40
  30.2 0.6 reshape.28
  30.8 12.0 %fusion.26 = f32[48,2048]{1,0:T(8,128)S(1)} fusion(bf16[48,7168]{1,0:T(8,128)(2,1)S(1)} %reshape.28, bf16[7168,2048]{1,0:T(8,128)(2,1)} %param.9), kind=kOutput, calls=%fused_computation.33 | convolution fusion | flops 1409286144 | bytes 30441472 | tf_op jit(solution)/shard_map/dot_general | solution.py:13
  42.9 0.0 copy-start.1
  42.9 0.0 copy-start.2
  42.9 20.8 %fusion.2 = f32[48,7168]{1,0:T(8,128)S(1)} fusion(bf16[2048,7168]{1,0:T(8,128)(2,1)} %param.11, bf16[48,7168]{1,0:T(8,128)(2,1)S(1)} %reshape.28, bf16[7168,2048]{1,0:T(8,128)(2,1)} %param.10, f32[48,2048]{1,0:T(8,128)S(1)} %fusion.26), kind=kOutput, calls=%fused_computation.5 | convolution fusion | flops 2819162112 | bytes 61177856 | tf_op jit(solution)/shard_map/dot_general | solution.py:16
  63.7 1.6 %reshape.29 = f32[16,3,7168]{2,1,0:T(4,128)} reshape(f32[48,7168]{1,0:T(8,128)S(1)} %fusion.2) | data formatting | bytes 2752512 | tf_op jit(solution)/shard_map/reshape | solution.py:17
  65.3 4.9 %all-to-all-start.1 = ((f32[16,3,7168]{2,1,0:T(4,128)}), f32[16,3,7168]{2,1,0:T(4,128)S(1)}, u32[]{:S(2)}, u32[]{:S(2)}) async-start(f32[16,3,7168]{2,1,0:T(4,128)} %reshape.29), calls=%async_computation.1 | async-start | bytes 3670016 | tf_op jit(solution)/shard_map/all_to_all | solution.py:45
  70.2 0.0 copy-done.1
  70.2 0.0 copy-done.2
  70.2 0.1 select_reduce_fusion
  70.3 41.7 %all-to-all-done.1 = f32[16,3,7168]{2,1,0:T(4,128)S(1)} async-done(((f32[16,3,7168]{2,1,0:T(4,128)}), f32[16,3,7168]{2,1,0:T(4,128)S(1)}, u32[]{:S(2)}, u32[]{:S(2)}) %all-to-all-start.1) | async-done | bytes 1376288 | tf_op jit(solution)/shard_map/all_to_all | solution.py:45
  112.0 2.1 %fusion = bf16[4,7168]{1,0:T(4,128)(2,1)} fusion(f32[16,3,7168]{2,1,0:T(4,128)S(1)} %all-to-all-done.1, f32[4,16]{1,0:T(4,128)S(1)} %select_reduce_fusion, s32[4,16]{1,0:T(4,128)S(1)} %convert_subtract_fusion, pred[4,16]{1,0:T(4,128)(4,1)S(1)} %get-tuple-element.5), kind=kOutput, calls=%fused_computation.2 | convolution fusion | flops 16544320 | bytes 1434176 | tf_op jit(solution)/shard_map/tec,ecd->td/dot_general | solution.py:47
  (3 shorter events, 0.1 us)
Async XLA Ops:
  0.0 0.8 copy-start
  42.9 27.3 %copy-start.1 = (s32[4,8]{1,0:T(4,128)S(1)}, s32[4,8]{1,0:T(4,128)}, u32[]{:S(2)}) copy-start(s32[4,8]{1,0:T(4,128)} %param.7) | copy-start | bytes 388
  42.9 27.3 %copy-start.2 = (f32[4,8]{1,0:T(4,128)S(1)}, f32[4,8]{1,0:T(4,128)}, u32[]{:S(2)}) copy-start(f32[4,8]{1,0:T(4,128)} %param.8) | copy-start | bytes 388
  65.3 46.7 %all-to-all-start.1 = ((f32[16,3,7168]{2,1,0:T(4,128)}), f32[16,3,7168]{2,1,0:T(4,128)S(1)}, u32[]{:S(2)}, u32[]{:S(2)}) async-start(f32[16,3,7168]{2,1,0:T(4,128)} %reshape.29), calls=%async_computation.1 | async-start | bytes 3670016 | tf_op jit(solution)/shard_map/all_to_all | solution.py:45
where the time goes:
time: 114 us
  waiting for transfers between devices  41.7 us (37%)
  matrix products  35.4 us (31%)
  blocking collectives  28.3 us (25%)
  starting transfers between devices  4.91 us (4%)
  local copies, waits for them, and re-layouts  2.81 us (2%)
    all_to_all x1, waiting for transfers between devices, shards(): lax.all_to_all(partial_value, 'ep', split_axis=0, concat_axis=0, tiled=True)  41.7 us
    all_to_all x1, blocking collectives, shards(): lax.all_to_all(outgoing, 'ep', split_axis=0, concat_axis=0, tiled=True)  28.3 us
    dot_general x1, matrix products, expert_forward(): result = jnp.dot(hidden, down_weight, preferred_element_type=jnp.float32)  20.8 us
    dot_general x1, matrix products, expert_forward(): jnp.dot(flat_rows, gate_weight, preferred_element_type=jnp.float32)  12 us
    all_to_all x1, starting transfers between devices, shards(): lax.all_to_all(partial_value, 'ep', split_axis=0, concat_axis=0, tiled=True)  4.91 us
  transfers between devices with their start and end apart: 1, of which 1 were waited for; matrix products, arithmetic and copies ran while one was open for 0% of the time, Pallas kernels for 0%

commit v1 on v0

v1 whole, which is shorter than its diff:
```python
import jax
import jax.numpy as jnp
from jax import lax
from jax.experimental import pallas as pl
from jax.experimental.pallas import tpu as pltpu
from jax.sharding import PartitionSpec as P


EXPERTS = 16
LANES = 128
UNIT = 512


def load_kernel(source, target, sems):
    count, _, unit = target.shape
    copies = [
        pltpu.make_async_copy(source.at[:, pl.ds(j * unit, unit)], target.at[j], sems.at[j])
        for j in range(count)
    ]
    for copy in copies:
        copy.start()
    for copy in copies:
        copy.wait()


def load_columns(weight, count):
    return pl.pallas_call(
        load_kernel,
        out_shape=pltpu.VMEM((count, weight.shape[0], UNIT), weight.dtype),
        in_specs=[pl.BlockSpec(memory_space=pltpu.HBM)],
        out_specs=pl.BlockSpec(memory_space=pltpu.VMEM),
        scratch_shapes=[pltpu.SemaphoreType.DMA((count,))],
        compiler_params=pltpu.CompilerParams(vmem_limit_bytes=1 << 20),
    )(weight)


def join_kernel(*refs):
    target = refs[-1]
    size = target.shape[0] // (len(refs) - 1)
    for i, part in enumerate(refs[:-1]):
        target[pl.ds(i * size, size)] = part[...]


def join(parts):
    vmem = pl.BlockSpec(memory_space=pltpu.VMEM)
    return pl.pallas_call(
        join_kernel,
        out_shape=pltpu.VMEM((sum(p.shape[0] for p in parts), parts[0].shape[1]), parts[0].dtype),
        in_specs=[vmem] * len(parts),
        out_specs=vmem,
        compiler_params=pltpu.CompilerParams(vmem_limit_bytes=2 << 20),
    )(*[pltpu.with_memory_space_constraint(part, pltpu.VMEM) for part in parts])


def gate_of(info, expert):
    lane = lax.broadcasted_iota(jnp.int32, info.shape, 1)
    return jnp.sum(jnp.where(lane % EXPERTS == expert, info.astype(jnp.float32), 0.0), axis=1, keepdims=True)


def expert_kernel(
    per_expert, pieces, gate_in, up_in, gate_hbm, down_hbm, send, keep, gate_held, up_held, rows, hidden, last_sem, sems
):
    del gate_in, up_in
    units, kept = up_held.shape[0], gate_held.shape[0]
    depth, width = down_hbm.shape
    half = send.shape[0]
    chunks = width // UNIT
    per_unit = gate_held.shape[1] // depth
    model = rows.shape[1]
    last = pltpu.make_async_copy(gate_hbm.at[:, pl.ds(kept * UNIT, UNIT)], gate_held.at[0], last_sem)
    freed = [(up_held, 0)] + [(held, j) for j in range(1, kept) for held in (gate_held, up_held)]

    def place(c):
        held, j = freed[c // per_unit]
        return held.at[j, pl.ds((c % per_unit) * depth, depth)]

    downs = [
        pltpu.make_async_copy(down_hbm.at[:, pl.ds(c * UNIT, UNIT)], place(c), sems.at[c])
        for c in range(chunks)
    ]
    info = []
    for i, piece in enumerate(pieces):
        rows[pl.ds(i * piece.shape[0], piece.shape[0])] = piece[:, :model]
        info.append(piece[:, model:])
    expert = lax.axis_index("ep") // per_expert
    gate = jnp.concatenate([gate_of(part, expert) for part in info], axis=0)
    started = 0
    for j in range(units):
        if j == kept:
            last.wait()
        x = rows[...]
        gate_act = jnp.dot(x, gate_held[j % kept], preferred_element_type=jnp.float32)
        up_act = jnp.dot(x, up_held[j], preferred_element_type=jnp.float32)
        value = gate_act / (1.0 + jnp.exp(-gate_act)) * up_act
        hidden[:, pl.ds(j * UNIT, UNIT)] = value.astype(hidden.dtype)
        if j == 0:
            last.start()
        for c in range(started, min((2 * j + 1) * per_unit, chunks)):
            downs[c].start()
            started = c + 1
    for c in range(chunks):
        downs[c].wait()
        part = jnp.dot(hidden[...], place(c)[...], preferred_element_type=jnp.float32) * gate
        keep[:, pl.ds(c * UNIT, UNIT)] = part[:half].astype(keep.dtype)
        send[:, pl.ds(c * UNIT, UNIT)] = part[half:].astype(send.dtype)


def run_expert(per_expert, pieces, gate_held, up_held, gate_weight, down_weight):
    count = len(pieces)
    total = sum(piece.shape[0] for piece in pieces)
    half, width = total // 2, down_weight.shape[1]

    def kernel(*refs):
        expert_kernel(per_expert, refs[:count], *refs[count:])

    vmem = pl.BlockSpec(memory_space=pltpu.VMEM)
    hbm = pl.BlockSpec(memory_space=pltpu.HBM)
    held = [pltpu.with_memory_space_constraint(piece, pltpu.VMEM) for piece in pieces]
    outs = pl.pallas_call(
        kernel,
        out_shape=(
            pltpu.VMEM((half, width), jnp.bfloat16),
            pltpu.VMEM((half, width), jnp.float32),
            pltpu.VMEM(gate_held.shape, gate_held.dtype),
            pltpu.VMEM(up_held.shape, up_held.dtype),
        ),
        in_specs=[vmem] * (count + 2) + [hbm, hbm],
        out_specs=(vmem,) * 4,
        input_output_aliases={count: 2, count + 1: 3},
        scratch_shapes=[
            pltpu.VMEM((total, gate_held.shape[1]), jnp.bfloat16),
            pltpu.VMEM((total, down_weight.shape[0]), jnp.bfloat16),
            pltpu.SemaphoreType.DMA,
            pltpu.SemaphoreType.DMA((width // UNIT,)),
        ],
        compiler_params=pltpu.CompilerParams(vmem_limit_bytes=3 << 20),
    )(*held, gate_held, up_held, gate_weight, down_weight)
    return outs[0], outs[1]


def plain_expert(per_expert, rows, gate_weight, up_weight, down_weight):
    model = gate_weight.shape[0]
    x = rows[:, :model]
    gate_act = jnp.dot(x, gate_weight, preferred_element_type=jnp.float32)
    up_act = jnp.dot(x, up_weight, preferred_element_type=jnp.float32)
    hidden = (jax.nn.silu(gate_act) * up_act).astype(jnp.bfloat16)
    part = jnp.dot(hidden, down_weight, preferred_element_type=jnp.float32)
    part = part * gate_of(rows[:, model:], lax.axis_index("ep") // per_expert)
    half = part.shape[0] // 2
    return part[half:].astype(jnp.bfloat16), part[:half]


def with_gates(tokens, routes, gates):
    member = routes[:, :, None] == jnp.arange(EXPERTS, dtype=jnp.int32)
    share = jnp.sum(jnp.where(member, gates[:, :, None], 0.0), axis=1)
    high = lax.reduce_precision(share, 8, 7)
    middle = lax.reduce_precision(share - high, 8, 7)
    low = share - high - middle
    parts = jnp.concatenate([high, middle, low], axis=1).astype(jnp.bfloat16)
    info = jnp.pad(parts, ((0, 0), (0, LANES - parts.shape[1])))
    return jnp.concatenate([tokens, info], axis=1)


def stages_of(devices):
    bits = []
    bit = devices // 2
    while bit >= 1:
        bits.append(bit)
        bit //= 2
    stages = []
    while len(bits) > 2:
        take = min(2, len(bits) - 2)
        group, bits = bits[:take], bits[take:]
        stages.append(tuple(sorted((sum(b for i, b in enumerate(group) if m >> i & 1) for m in range(1, 2 ** len(group))), reverse=True)))
    return stages + [(b,) for b in bits]


def shards(tokens, routes, gates, gate_weight, up_weight, down_weight):
    devices = lax.axis_size("ep")
    per_expert = devices // EXPERTS

    def swap(x, offset):
        return lax.ppermute(x, "ep", [(i, i ^ offset) for i in range(devices)])

    stages = stages_of(devices)
    depth, hidden = gate_weight.shape[0], gate_weight.shape[1]
    units = hidden // UNIT
    fast = hidden == 4 * UNIT and devices * tokens.shape[0] <= 64 and depth % UNIT == 0
    rows = with_gates(tokens, routes, gates)
    for offsets in stages[:-2]:
        parts = [rows] + [swap(rows, offset) for offset in offsets]
        rows = join(parts) if fast else jnp.concatenate(parts, axis=0)
    pieces = [rows, swap(rows, stages[-2][0])]
    pieces += [swap(piece, stages[-1][0]) for piece in pieces]
    if fast:
        gate_weight, up_weight, down_weight = (
            pltpu.with_memory_space_constraint(w, pltpu.HBM) for w in (gate_weight, up_weight, down_weight)
        )
        gate_held = load_columns(gate_weight, units - 1)
        up_held = load_columns(up_weight, units)
        send, keep = run_expert(per_expert, pieces, gate_held, up_held, gate_weight, down_weight)
    else:
        rows = jnp.concatenate(pieces, axis=0)
        send, keep = plain_expert(per_expert, rows, gate_weight, up_weight, down_weight)
    keep = keep + swap(send, stages[-1][0]).astype(jnp.float32)
    for offsets in stages[-2::-1]:
        size = keep.shape[0] // (len(offsets) + 1)
        got = [
            swap(keep[(i + 1) * size : (i + 2) * size].astype(jnp.bfloat16), offset)
            for i, offset in enumerate(offsets)
        ]
        keep = keep[:size] + sum(part.astype(jnp.float32) for part in got)
    return keep.astype(jnp.bfloat16)


def solution(mesh):
    placed = (
        P(("groups", "ep"), None),
        P(("groups", "ep"), None),
        P(("groups", "ep"), None),
        P(None, "ep"),
        P(None, "ep"),
        P("ep", None),
    )

    return jax.shard_map(shards, mesh=mesh, in_specs=placed, out_specs=P(("groups", "ep"), None), check_vma=False)
```

time: 114 us -> 71.9 us (0.63)
  the two profiles are of different devices: /device:TPU:15 before, /device:TPU:0 now
where the time goes in v1:
time: 71.9 us; the launch traced here: 71.7 us
  Pallas kernels  34.1 us (47%)
  waiting for transfers between devices  21.1 us (29%)
  starting transfers between devices  13.9 us (19%)
  other arithmetic  2.54 us (4%)
    ppermute x11, waiting for transfers between devices, swap(): return lax.ppermute(x, 'ep', [(i, i ^ offset) for i in range(devices)])  21.1 us
    pallas_call x1, Pallas kernels, run_expert(): pl.pallas_call(kernel, out_shape=(pltpu.VMEM((half, width), jnp.bfloat16)...  17.2 us
    pallas_call x2, Pallas kernels, load_columns(): pl.pallas_call(load_kernel, out_shape=pltpu.VMEM((count, weight.shape[0],...  16.8 us
    ppermute x11, starting transfers between devices, swap(): return lax.ppermute(x, 'ep', [(i, i ^ offset) for i in range(devices)])  13.9 us
  transfers between devices with their start and end apart: 11, of which 7 were waited for; matrix products, arithmetic and copies ran while one was open for 0% of the time, Pallas kernels for 23%

profile of v1, /device:TPU:0, one launch (start us, length us, event | category | flops | bytes accessed | tf_op | source)
XLA Modules:
  0.0 71.7 jit_solution(9111871501471075819)
XLA Ops:
  0.0 0.8 %select_reduce_fusion = f32[4,16]{1,0:T(4,128)S(1)} fusion(f32[4,8]{1,0:T(4,128)} %param.8, s32[4,8]{1,0:T(4,128)} %param.7), kind=kLoop, calls=%fused_computation.6 | loop fusion | flops 1472 | bytes 512 | tf_op jit(solution)/shard_map/reduce_sum | solution.py:155
  0.8 0.1 fusion.6
  0.9 0.8 %pad_maximum_fusion.refs_0_ = bf16[4,7296]{1,0:T(4,128)(2,1)S(1)} fusion(bf16[4,128]{1,0:T(4,128)(2,1)S(1)} %fusion.6, bf16[4,7168]{1,0:T(4,128)(2,1)} %param.6), kind=kLoop, calls=%fused_computation.5 | loop fusion | flops 116736 | bytes 116736 | tf_op jit(solution)/shard_map/concatenate | solution.py:161
  1.7 3.1 %collective-permute-start.2 = (bf16[4,7296]{1,0:T(4,128)(2,1)S(1)}, bf16[4,7296]{1,0:T(4,128)(2,1)S(1)}, u32[]{:S(2)}, u32[]{:S(2)}) collective-permute-start(bf16[4,7296]{1,0:T(4,128)(2,1)S(1)} %pad_maximum_fusion.refs_0_), channel_id=1, source_target_pairs={{0,4},{1,5},{2,6},{3,7},{4,0},{5,1},{6,2},{7,3},{8,12},{9,13},{10,... | collective-permute-start | bytes 175112 | tf_op jit(solution)/shard_map/ppermute | solution.py:183
  4.8 2.6 %collective-permute-start.1 = (bf16[4,7296]{1,0:T(4,128)(2,1)S(1)}, bf16[4,7296]{1,0:T(4,128)(2,1)S(1)}, u32[]{:S(2)}, u32[]{:S(2)}) collective-permute-start(bf16[4,7296]{1,0:T(4,128)(2,1)S(1)} %pad_maximum_fusion.refs_0_), channel_id=1, source_target_pairs={{0,8},{1,9},{2,10},{3,11},{4,12},{5,13},{6,14},{7,15},{8,0},{9,1},... | collective-permute-start | bytes 175112 | tf_op jit(solution)/shard_map/ppermute | solution.py:183
  7.4 3.6 %collective-permute-done.1.refs_2_ = bf16[4,7296]{1,0:T(4,128)(2,1)S(1)} collective-permute-done((bf16[4,7296]{1,0:T(4,128)(2,1)S(1)}, bf16[4,7296]{1,0:T(4,128)(2,1)S(1)}, u32[]{:S(2)}, u32[]{:S(2)}) %collective-permute-start.1) | collective-permute-done | bytes 58400 | tf_op jit(solution)/shard_map/ppermute | solution.py:183
  11.1 2.4 %collective-permute-done.refs_1_ = bf16[4,7296]{1,0:T(4,128)(2,1)S(1)} collective-permute-done((bf16[4,7296]{1,0:T(4,128)(2,1)S(1)}, bf16[4,7296]{1,0:T(4,128)(2,1)S(1)}, u32[]{:S(2)}, u32[]{:S(2)}) %collective-permute-start) | collective-permute-done | bytes 58400 | tf_op jit(solution)/shard_map/ppermute | solution.py:183
  13.5 1.6 %collective-permute-start.3 = (bf16[16,7296]{1,0:T(8,128)(2,1)S(1)}, bf16[16,7296]{1,0:T(8,128)(2,1)S(1)}, u32[]{:S(2)}, u32[]{:S(2)}) collective-permute-start(bf16[16,7296]{1,0:T(8,128)(2,1)S(1)} %shard_map.64.refs_0_), channel_id=1, source_target_pairs={{0,2},{1,3},{2,0},{3,1},{4,6},{5,7},{6,4},{7,5},{8,10},{9,11},{10,... | collective-permute-start | bytes 700424 | tf_op jit(solution)/shard_map/ppermute | solution.py:183
  15.0 4.6 %collective-permute-done.3.refs_1_ = bf16[16,7296]{1,0:T(8,128)(2,1)S(1)} collective-permute-done((bf16[16,7296]{1,0:T(8,128)(2,1)S(1)}, bf16[16,7296]{1,0:T(8,128)(2,1)S(1)}, u32[]{:S(2)}, u32[]{:S(2)}) %collective-permute-start.3) | collective-permute-done | bytes 233504 | tf_op jit(solution)/shard_map/ppermute | solution.py:183
  19.6 7.4 %shard_map.65.refs_4_ = bf16[3,7168,512]{2,1,0:T(8,128)(2,1)S(1)} custom-call(bf16[7168,2048]{1,0:T(8,128)(2,1)} %refs_6_.1), custom_call_target="tpu_custom_call" | custom-call | tf_op jit(solution)/shard_map/pallas_call | solution.py:27
  27.0 9.4 %shard_map.66.refs_5_ = bf16[4,7168,512]{2,1,0:T(8,128)(2,1)S(1)} custom-call(bf16[7168,2048]{1,0:T(8,128)(2,1)} %source.3), custom_call_target="tpu_custom_call" | custom-call | tf_op jit(solution)/shard_map/pallas_call | solution.py:27
  36.5 17.2 %shard_map.67 = (bf16[32,7168]{1,0:T(8,128)(2,1)S(1)}, f32[32,7168]{1,0:T(8,128)S(1)}, bf16[3,7168,512]{2,1,0:T(8,128)(2,1)S(1)}, bf16[4,7168,512]{2,1,0:T(8,128)(2,1)S(1)}) custom-call(bf16[16,7296]{1,0:T(8,128)(2,1)S(1)} %shard_map.64.refs_0_, bf16[16,7296]{1,0:T(8,128)(2,1)S(1)} %collective-permute-done.3.refs_1_, ...), custom_call_target="tpu_custom_call", output_to_operand_aliasing={{2}: (4, {}), {3}: (5, {})} | custom-call | tf_op jit(solution)/shard_map/pallas_call | solution.py:119
  53.7 0.6 collective-permute-start.6
  54.3 1.4 %collective-permute-done.6 = bf16[32,7168]{1,0:T(8,128)(2,1)S(1)} collective-permute-done((bf16[32,7168]{1,0:T(8,128)(2,1)S(1)}, bf16[32,7168]{1,0:T(8,128)(2,1)S(1)}, u32[]{:S(2)}, u32[]{:S(2)}) %collective-permute-start.6) | collective-permute-done | bytes 458784 | tf_op jit(solution)/shard_map/ppermute | solution.py:183
  55.7 0.1 convert_add_fusion
  55.8 1.6 %collective-permute-start.7 = (bf16[16,7168]{1,0:T(8,128)(2,1)S(1)}, bf16[16,7168]{1,0:T(8,128)(2,1)S(1)}, u32[]{:S(2)}, u32[]{:S(2)}) collective-permute-start(bf16[16,7168]{1,0:T(8,128)(2,1)S(1)} %slice.39), channel_id=1, source_target_pairs={{0,2},{1,3},{2,0},{3,1},{4,6},{5,7},{6,4},{7,5},{8,10},{9,11},{10,... | collective-permute-start | bytes 688136 | tf_op jit(solution)/shard_map/ppermute | solution.py:183
  57.4 6.4 %collective-permute-done.7 = bf16[16,7168]{1,0:T(8,128)(2,1)S(1)} collective-permute-done((bf16[16,7168]{1,0:T(8,128)(2,1)S(1)}, bf16[16,7168]{1,0:T(8,128)(2,1)S(1)}, u32[]{:S(2)}, u32[]{:S(2)}) %collective-permute-start.7) | collective-permute-done | bytes 229408 | tf_op jit(solution)/shard_map/ppermute | solution.py:183
  63.8 0.1 fusion.8
  63.9 1.4 %collective-permute-start.8 = (bf16[4,7168]{1,0:T(4,128)(2,1)S(1)}, bf16[4,7168]{1,0:T(4,128)(2,1)S(1)}, u32[]{:S(2)}, u32[]{:S(2)}) collective-permute-start(bf16[4,7168]{1,0:T(4,128)(2,1)S(1)} %get-tuple-element.11), channel_id=1, source_target_pairs={{0,12},{1,13},{2,14},{3,15},{4,8},{5,9},{6,10},{7,11},{8,4},{9,5},... | collective-permute-start | bytes 172040 | tf_op jit(solution)/shard_map/ppermute | solution.py:183
  65.3 0.5 collective-permute-start.10
  65.8 2.5 %collective-permute-start.9 = (bf16[4,7168]{1,0:T(4,128)(2,1)S(1)}, bf16[4,7168]{1,0:T(4,128)(2,1)S(1)}, u32[]{:S(2)}, u32[]{:S(2)}) collective-permute-start(bf16[4,7168]{1,0:T(4,128)(2,1)S(1)} %get-tuple-element.13), channel_id=1, source_target_pairs={{0,8},{1,9},{2,10},{3,11},{4,12},{5,13},{6,14},{7,15},{8,0},{9,1},... | collective-permute-start | bytes 172040 | tf_op jit(solution)/shard_map/ppermute | solution.py:183
  68.4 2.1 %collective-permute-done.8 = bf16[4,7168]{1,0:T(4,128)(2,1)S(1)} collective-permute-done((bf16[4,7168]{1,0:T(4,128)(2,1)S(1)}, bf16[4,7168]{1,0:T(4,128)(2,1)S(1)}, u32[]{:S(2)}, u32[]{:S(2)}) %collective-permute-start.8) | collective-permute-done | bytes 57376 | tf_op jit(solution)/shard_map/ppermute | solution.py:183
  70.5 0.6 collective-permute-done.9
  71.1 0.7 fusion
  (11 shorter events, 0.2 us)
Async XLA Ops:
  1.7 5.7 %collective-permute-start.2 = (bf16[4,7296]{1,0:T(4,128)(2,1)S(1)}, bf16[4,7296]{1,0:T(4,128)(2,1)S(1)}, u32[]{:S(2)}, u32[]{:S(2)}) collective-permute-start(bf16[4,7296]{1,0:T(4,128)(2,1)S(1)} %pad_maximum_fusion.refs_0_), channel_id=1, source_target_pairs={{0,4},{1,5},{2,6},{3,7},{4,0},{5,1},{6,2},{7,3},{8,12},{9,13},{10,... | collective-permute-start | bytes 175112 | tf_op jit(solution)/shard_map/ppermute | solution.py:183
  4.8 6.2 %collective-permute-start.1 = (bf16[4,7296]{1,0:T(4,128)(2,1)S(1)}, bf16[4,7296]{1,0:T(4,128)(2,1)S(1)}, u32[]{:S(2)}, u32[]{:S(2)}) collective-permute-start(bf16[4,7296]{1,0:T(4,128)(2,1)S(1)} %pad_maximum_fusion.refs_0_), channel_id=1, source_target_pairs={{0,8},{1,9},{2,10},{3,11},{4,12},{5,13},{6,14},{7,15},{8,0},{9,1},... | collective-permute-start | bytes 175112 | tf_op jit(solution)/shard_map/ppermute | solution.py:183
  7.4 6.0 %collective-permute-start = (bf16[4,7296]{1,0:T(4,128)(2,1)S(1)}, bf16[4,7296]{1,0:T(4,128)(2,1)S(1)}, u32[]{:S(2)}, u32[]{:S(2)}) collective-permute-start(bf16[4,7296]{1,0:T(4,128)(2,1)S(1)} %pad_maximum_fusion.refs_0_), channel_id=1, source_target_pairs={{0,12},{1,13},{2,14},{3,15},{4,8},{5,9},{6,10},{7,11},{8,4},{9,5},... | collective-permute-start | bytes 175112 | tf_op jit(solution)/shard_map/ppermute | solution.py:183
  13.5 6.1 %collective-permute-start.3 = (bf16[16,7296]{1,0:T(8,128)(2,1)S(1)}, bf16[16,7296]{1,0:T(8,128)(2,1)S(1)}, u32[]{:S(2)}, u32[]{:S(2)}) collective-permute-start(bf16[16,7296]{1,0:T(8,128)(2,1)S(1)} %shard_map.64.refs_0_), channel_id=1, source_target_pairs={{0,2},{1,3},{2,0},{3,1},{4,6},{5,7},{6,4},{7,5},{8,10},{9,11},{10,... | collective-permute-start | bytes 700424 | tf_op jit(solution)/shard_map/ppermute | solution.py:183
  15.0 21.4 %collective-permute-start.4 = (bf16[16,7296]{1,0:T(8,128)(2,1)S(1)}, bf16[16,7296]{1,0:T(8,128)(2,1)S(1)}, u32[]{:S(2)}, u32[]{:S(2)}) collective-permute-start(bf16[16,7296]{1,0:T(8,128)(2,1)S(1)} %shard_map.64.refs_0_), channel_id=1, source_target_pairs={{0,1},{1,0},{2,3},{3,2},{4,5},{5,4},{6,7},{7,6},{8,9},{9,8},{10,11... | collective-permute-start | bytes 700424 | tf_op jit(solution)/shard_map/ppermute | solution.py:183
  19.6 16.9 %collective-permute-start.5 = (bf16[16,7296]{1,0:T(8,128)(2,1)S(1)}, bf16[16,7296]{1,0:T(8,128)(2,1)S(1)}, u32[]{:S(2)}, u32[]{:S(2)}) collective-permute-start(bf16[16,7296]{1,0:T(8,128)(2,1)S(1)} %collective-permute-done.3.refs_1_), channel_id=1, source_target_pairs={{0,1},{1,0},{2,3},{3,2},{4,5},{5,4},{6,7},{7,6},{8,9},{9,8},{10,11... | collective-permute-start | bytes 700424 | tf_op jit(solution)/shard_map/ppermute | solution.py:183
  53.7 2.0 %collective-permute-start.6 = (bf16[32,7168]{1,0:T(8,128)(2,1)S(1)}, bf16[32,7168]{1,0:T(8,128)(2,1)S(1)}, u32[]{:S(2)}, u32[]{:S(2)}) collective-permute-start(bf16[32,7168]{1,0:T(8,128)(2,1)S(1)} %get-tuple-element.8), channel_id=1, source_target_pairs={{0,1},{1,0},{2,3},{3,2},{4,5},{5,4},{6,7},{7,6},{8,9},{9,8},{10,11... | collective-permute-start | bytes 1376264 | tf_op jit(solution)/shard_map/ppermute | solution.py:183
  55.8 7.9 %collective-permute-start.7 = (bf16[16,7168]{1,0:T(8,128)(2,1)S(1)}, bf16[16,7168]{1,0:T(8,128)(2,1)S(1)}, u32[]{:S(2)}, u32[]{:S(2)}) collective-permute-start(bf16[16,7168]{1,0:T(8,128)(2,1)S(1)} %slice.39), channel_id=1, source_target_pairs={{0,2},{1,3},{2,0},{3,1},{4,6},{5,7},{6,4},{7,5},{8,10},{9,11},{10,... | collective-permute-start | bytes 688136 | tf_op jit(solution)/shard_map/ppermute | solution.py:183
  63.9 6.5 %collective-permute-start.8 = (bf16[4,7168]{1,0:T(4,128)(2,1)S(1)}, bf16[4,7168]{1,0:T(4,128)(2,1)S(1)}, u32[]{:S(2)}, u32[]{:S(2)}) collective-permute-start(bf16[4,7168]{1,0:T(4,128)(2,1)S(1)} %get-tuple-element.11), channel_id=1, source_target_pairs={{0,12},{1,13},{2,14},{3,15},{4,8},{5,9},{6,10},{7,11},{8,4},{9,5},... | collective-permute-start | bytes 172040 | tf_op jit(solution)/shard_map/ppermute | solution.py:183
  65.3 5.2 %collective-permute-start.10 = (bf16[4,7168]{1,0:T(4,128)(2,1)S(1)}, bf16[4,7168]{1,0:T(4,128)(2,1)S(1)}, u32[]{:S(2)}, u32[]{:S(2)}) collective-permute-start(bf16[4,7168]{1,0:T(4,128)(2,1)S(1)} %get-tuple-element.12), channel_id=1, source_target_pairs={{0,4},{1,5},{2,6},{3,7},{4,0},{5,1},{6,2},{7,3},{8,12},{9,13},{10,... | collective-permute-start | bytes 172040 | tf_op jit(solution)/shard_map/ppermute | solution.py:183
  65.8 5.2 %collective-permute-start.9 = (bf16[4,7168]{1,0:T(4,128)(2,1)S(1)}, bf16[4,7168]{1,0:T(4,128)(2,1)S(1)}, u32[]{:S(2)}, u32[]{:S(2)}) collective-permute-start(bf16[4,7168]{1,0:T(4,128)(2,1)S(1)} %get-tuple-element.13), channel_id=1, source_target_pairs={{0,8},{1,9},{2,10},{3,11},{4,12},{5,13},{6,14},{7,15},{8,0},{9,1},... | collective-permute-start | bytes 172040 | tf_op jit(solution)/shard_map/ppermute | solution.py:183
